TPU v7x, 32 devices: a whole 2x2x4 slice. The times are simulated.
32 devices in a mesh: cell: 16 (over z, y, x), gene: 2 (over core).
Axes of the slice: x: 2, y: 2, z: 4, core: 2. Of those that a mesh axis runs over, the one named last changes fastest.
Arguments:
- tiles: bfloat16 [2, 1024, 128, 128], P('gene', 'cell'), may hold values from -8 to 8
- tile_row: int32 [2, 1024], P('gene', 'cell'), may hold values from 0 to 7, as said below
- tile_col: int32 [2, 1024], P('gene', 'cell'), may hold values from 0 to 15
- tile_count: int32 [2, 16], P('gene', 'cell'), may hold values from 1 to 64, as said below
- start_basis: bfloat16 [64, 4096], P(None, 'gene'), may hold values from -0.09375 to 0.09375
Outputs:
- basis: bfloat16 [64, 16384], P(None, 'cell')
- loadings: float32 [64, 4096], P(None, ('gene', 'cell'))
Inputs may be any that keep to these rules, and one draw needn't show every extreme that they name: `tile_row`: tile row of each slot, within 0 to 7; the slots of one device name distinct (row, column) pairs. `tile_count`: slots in use; for each index of gene some device uses all 64.
All inputs are finite; a program needn't handle non-finite values.
Results may differ from a plain program's by a relative error of at most 0.018.
Values may be sent and summed in bfloat16 or wider, within the bound.
No kernel may reach another device: no remote copies, remote signals or barrier semaphores. Data moves between devices by JAX's collectives and lax.ppermute only.
A program may use at most 64 MiB of HBM per device.

v0:
```python
import jax
import jax.numpy as jnp
from jax import lax
from jax.sharding import PartitionSpec as P

ROW_BLOCKS = 8


def solve_lower(lower, right):
    return lax.linalg.triangular_solve(lower, right, left_side=True, lower=True)


def gram_of(scores):
    return jnp.dot(
        scores, scores.T, precision=lax.Precision.HIGHEST, preferred_element_type=jnp.float32
    )


def orthonormal(scores, first_total):
    first = first_total(gram_of(scores))
    lower_one = jnp.linalg.cholesky(first)
    return solve_lower(lower_one, scores)


def local(tiles, tile_row, tile_col, tile_count, start_basis):
    blocks_local = tiles[0]
    slot_count = blocks_local.shape[0]
    tile_size = blocks_local.shape[-1]
    width = start_basis.shape[0]
    gene_dev = start_basis.shape[1]
    gene_blocks = gene_dev // tile_size
    row_blocks = ROW_BLOCKS
    cell_dev = row_blocks * tile_size
    row_index = tile_row[0]
    col_index = tile_col[0]
    live = jnp.arange(slot_count) < tile_count[0, 0]
    row_target = jnp.where(live, row_index, row_blocks)
    col_target = jnp.where(live, col_index, gene_blocks)

    def first_total(gram):
        return lax.psum(gram, ("cell", "gene"))

    def merge_halves(partial_scores):
        return lax.psum_scatter(partial_scores, "gene", scatter_dimension=1, tiled=True)

    def scores_of(basis):
        picked = jnp.take(basis.reshape(width, gene_blocks, tile_size), col_index, axis=1)
        products = jnp.einsum(
            "ksg,srg->skr", picked, blocks_local, preferred_element_type=jnp.float32
        )
        summed = jax.ops.segment_sum(products, row_target, num_segments=row_blocks + 1)[:row_blocks]
        return merge_halves(jnp.transpose(summed, (1, 0, 2)).reshape(width, cell_dev))

    def loadings_of(ortho_half):
        picked = jnp.take(ortho_half.reshape(width, row_blocks, tile_size), row_index, axis=1)
        products = jnp.einsum(
            "ksr,srg->skg", picked, blocks_local, preferred_element_type=jnp.float32
        )
        summed = jax.ops.segment_sum(products, col_target, num_segments=gene_blocks + 1)[
            :gene_blocks
        ]
        return jnp.transpose(summed, (1, 0, 2)).reshape(width, gene_dev)

    ortho = orthonormal(scores_of(start_basis), first_total)
    ortho_half = ortho.astype(jnp.bfloat16)
    ortho_rows = lax.all_gather(ortho_half, "gene", axis=1, tiled=True)
    partial_value = loadings_of(ortho_rows)
    next_basis = lax.psum(partial_value, "cell").astype(jnp.bfloat16)
    ortho_two = orthonormal(scores_of(next_basis), first_total)
    scale = jnp.sqrt(jnp.float32(lax.axis_size("cell") * cell_dev))
    ortho_two_half = ortho_two.astype(jnp.bfloat16)
    basis_piece = (ortho_two * scale).astype(jnp.bfloat16)
    final_rows, basis = (
        lax.all_gather(ortho_two_half, "gene", axis=1, tiled=True),
        lax.all_gather(basis_piece, "gene", axis=1, tiled=True),
    )
    loadings = lax.psum_scatter(loadings_of(final_rows), "cell", scatter_dimension=1, tiled=True)
    return (basis, loadings)


def solution(mesh):
    return jax.shard_map(
        local,
        mesh=mesh,
        in_specs=(
            P("gene", "cell", None, None),
            P("gene", "cell"),
            P("gene", "cell"),
            P("gene", "cell"),
            P(None, "gene"),
        ),
        out_specs=(P(None, "cell"), P(None, ("gene", "cell"))),
        check_vma=False,
    )
```

profile of v0, /device:TPU:0, one launch (start us, length us, event | category | flops | bytes accessed | tf_op | source)
XLA Modules:
  0.0 349.9 jit_solution(15291023441210544630)
XLA Ops:
  11.2 2.9 fusion.6
  14.1 7.1 %scatter_fusion = f32[9,64,128]{2,1,0:T(8,128)S(1)} fusion(f32[9,64,128]{2,1,0:T(8,128)S(1)} %broadcast.69.clone, s32[64]{0:T(128)S(1)} %get-tuple-element.8, f32[64,64,128]{2,1,0:T(8,128)} %fusion.6), kind=kCustom, calls=%fused_computation.4 | custom fusion | flops 524288 | bytes 6291712 | tf_op jit(solution)/shard_map/scatter-add | solution.py:51
  22.0 10.5 %reduce-scatter.4.cloned.1.call-done = f32[64,512]{1,0:T(8,128)} async-done(((f32[64,1024]{1,0:T(8,128)}), f32[64,512]{1,0:T(8,128)}) %reduce-scatter.4.cloned.1.call-update) | async-done | bytes 131088 | tf_op jit(solution)/shard_map/reduce_scatter | solution.py:44
  32.5 1.2 fusion.40
  33.8 40.5 %psum.21 = f32[64,64]{0,1:T(8,128)S(1)} all-reduce(f32[64,64]{0,1:T(8,128)S(1)} %fusion.40), channel_id=1, replica_groups=mesh['cell'=16,'gene'=2] {'cell','gene'}, use_global_device_ids=true, to_apply=%region_2.4 | all-reduce | flops 4096 | bytes 32768 | tf_op jit(solution)/shard_map/psum | solution.py:41
  74.4 5.8 %cholesky.44 = f32[64,64]{1,0:T(8,128)S(1)} custom-call(f32[64,64]{1,0:T(8,128)S(1)} %fusion.30), custom_call_target="Cholesky" | custom-call | tf_op jit(solution)/shard_map/jit(cholesky)/cholesky | solution.py:21
  81.6 4.9 %custom-call.6 = f32[1,64,64]{1,2,0:T(8,128)S(1)} custom-call(f32[1,64,64]{2,1,0:T(8,128)S(1)} %fusion.24), custom_call_target="InvertDiagBlocksLowerTriangular" | custom-call | tf_op jit(solution)/shard_map/triangular_solve/custom-call.0 | solution.py:10
  86.5 1.2 convolution_convert_fusion
  87.7 1.9 all_gather.9
  90.4 2.1 fusion.4
  92.6 7.1 %scatter_fusion.1 = f32[17,64,128]{2,1,0:T(8,128)S(1)} fusion(f32[17,64,128]{2,1,0:T(8,128)S(1)} %broadcast.70.clone, s32[64]{0:T(128)S(1)} %get-tuple-element.9, f32[64,64,128]{2,1,0:T(8,128)} %fusion.4), kind=kCustom, calls=%fused_computation.5 | custom fusion | flops 524288 | bytes 6291712 | tf_op jit(solution)/shard_map/scatter-add | solution.py:59
  99.7 81.7 %all-reduce.1 = bf16[64,2048]{1,0:T(8,128)(2,1)S(1)} all-reduce(f32[64,2048]{1,0:T(8,128)S(1)} %copy_bitcast_fusion.1), channel_id=1, replica_groups=mesh['cell'=16,'gene'=2] {'cell'}, use_global_device_ids=true, to_apply=%region_6.11 | all-reduce | flops 131072 | bytes 786432 | tf_op jit(solution)/shard_map/psum | solution.py:68
  182.2 2.9 fusion.2
  185.1 7.1 %scatter_fusion.2 = f32[9,64,128]{2,1,0:T(8,128)S(1)} fusion(f32[9,64,128]{2,1,0:T(8,128)S(1)} %broadcast.69, s32[64]{0:T(128)S(1)} %get-tuple-element.8, f32[64,64,128]{2,1,0:T(8,128)} %fusion.2), kind=kCustom, calls=%fused_computation.6 | custom fusion | flops 524288 | bytes 6291712 | tf_op jit(solution)/shard_map/scatter-add | solution.py:51
  192.9 4.2 %reduce-scatter.6.cloned.1.call-done = f32[64,512]{1,0:T(8,128)} async-done(((f32[64,1024]{1,0:T(8,128)}), f32[64,512]{1,0:T(8,128)}) %reduce-scatter.6.cloned.1.call-update) | async-done | bytes 131088 | tf_op jit(solution)/shard_map/reduce_scatter | solution.py:44
  198.4 40.8 %psum.23 = f32[64,64]{0,1:T(8,128)S(1)} all-reduce(f32[64,64]{0,1:T(8,128)S(1)} %fusion.41), channel_id=1, replica_groups=mesh['cell'=16,'gene'=2] {'cell','gene'}, use_global_device_ids=true, to_apply=%region_9.14 | all-reduce | flops 4096 | bytes 32768 | tf_op jit(solution)/shard_map/psum | solution.py:41
  239.2 5.8 %cholesky.55 = f32[64,64]{1,0:T(8,128)S(1)} custom-call(f32[64,64]{1,0:T(8,128)S(1)} %fusion.28), custom_call_target="Cholesky" | custom-call | tf_op jit(solution)/shard_map/jit(cholesky)/cholesky | solution.py:21
  246.4 4.9 %custom-call.7 = f32[1,64,64]{1,2,0:T(8,128)S(1)} custom-call(f32[1,64,64]{2,1,0:T(8,128)S(1)} %fusion.25), custom_call_target="InvertDiagBlocksLowerTriangular" | custom-call | tf_op jit(solution)/shard_map/triangular_solve/custom-call.0 | solution.py:10
  251.3 1.2 fusion.39
  252.6 1.9 all_gather.11
  255.2 2.1 fusion
  257.4 7.1 %scatter_fusion.3 = f32[17,64,128]{2,1,0:T(8,128)S(1)} fusion(f32[17,64,128]{2,1,0:T(8,128)S(1)} %broadcast.70, s32[64]{0:T(128)S(1)} %get-tuple-element.9, f32[64,64,128]{2,1,0:T(8,128)} %fusion), kind=kCustom, calls=%fused_computation.7 | custom fusion | flops 524288 | bytes 6291712 | tf_op jit(solution)/shard_map/scatter-add | solution.py:59
  265.3 1.9 all_gather.10
  267.2 75.5 %reduce-scatter.8.cloned.1.call-done = f32[64,128]{1,0:T(8,128)} async-done(((f32[64,2048]{1,0:T(8,128)}), f32[64,128]{1,0:T(8,128)}) %reduce-scatter.8.cloned.1.call-update) | async-done | bytes 32784 | tf_op jit(solution)/shard_map/reduce_scatter | solution.py:77
  (47 shorter events, 12.9 us)
Async XLA Ops:
  7.2 4.0 %copy-start = (bf16[1,64,128,128]{3,2,1,0:T(8,128)(2,1)S(1)}, bf16[1,64,128,128]{3,2,1,0:T(8,128)(2,1)}, u32[]{:S(2)}) copy-start(bf16[1,64,128,128]{3,2,1,0:T(8,128)(2,1)} %param.12) | copy-start | bytes 6291460
  7.2 4.0 %copy-start.1 = (s32[1,64]{1,0:T(1,128)S(1)}, s32[1,64]{1,0:T(1,128)}, u32[]{:S(2)}) copy-start(s32[1,64]{1,0:T(1,128)} %param.14) | copy-start | bytes 772
  7.2 4.0 %copy-start.2 = (s32[1,64]{1,0:T(1,128)S(1)}, s32[1,64]{1,0:T(1,128)}, u32[]{:S(2)}) copy-start(s32[1,64]{1,0:T(1,128)} %param.13) | copy-start | bytes 772
  7.2 25.3 %reduce-scatter.4.cloned.1.call-start = ((), (), s32[]{:S(2)}) async-start(), calls=%async_computation.3 | async-start | bytes 393216 | tf_op jit(solution)/shard_map/reduce_scatter | solution.py:44
  21.9 175.2 %reduce-scatter.6.cloned.1.call-start = ((), (), s32[]{:S(2)}) async-start(), calls=%async_computation.4 | async-start | bytes 393216 | tf_op jit(solution)/shard_map/reduce_scatter | solution.py:44
  192.9 149.8 %reduce-scatter.8.cloned.1.call-start = ((), (), s32[]{:S(2)}) async-start(), calls=%async_computation.5 | async-start | bytes 557056 | tf_op jit(solution)/shard_map/reduce_scatter | solution.py:77
Sparse Core Ops, SparseCore 0:
  22.0 10.4 reduce-scatter.3
  193.0 4.0 reduce-scatter.5
  265.4 77.2 reduce-scatter.7
where the time goes:
time: 351 us; the launch traced here: 350 us
  blocking collectives  169 us (48%)
  waiting for transfers between devices  90.3 us (26%)
  other arithmetic  53.9 us (15%)
  matrix products  14.9 us (4%)
  between operations  14.7 us (4%)
  local copies, waits for them, and re-layouts  7.35 us (2%)
    psum x1, blocking collectives, local(): next_basis = lax.psum(partial_value, 'cell').astype(jnp.bfloat16)  81.7 us
    psum x2, blocking collectives, first_total(): return lax.psum(gram, ('cell', 'gene'))  81.3 us
    reduce_scatter x1, waiting for transfers between devices, local(): lax.psum_scatter(loadings_of(final_rows), 'cell', scatter_dimension=1, ti...  75.5 us
    reduce_scatter x2, waiting for transfers between devices, merge_halves(): lax.psum_scatter(partial_scores, 'gene', scatter_dimension=1, tiled=True)  14.7 us
    scatter-add x2, other arithmetic, scores_of(): jax.ops.segment_sum(products, row_target, num_segments=row_blocks + 1)  14.1 us
    scatter-add x2, other arithmetic, loadings_of(): jax.ops.segment_sum(products, col_target, num_segments=gene_blocks + 1)  14.1 us
    another operation x6, other arithmetic, orthonormal(): lower_one = jnp.linalg.cholesky(first)  13 us
    another operation x4, other arithmetic, solve_lower(): return lax.linalg.triangular_solve(lower, right, left_side=True, lower=True)  11.1 us
  transfers between devices with their start and end apart: 3, of which 3 were waited for; matrix products, arithmetic and copies ran while one was open for 0% of the time, Pallas kernels for 0%

commit v1 on v0

--- a/solution.py
+++ b/solution.py
@@ -65,7 +65,11 @@
     ortho_half = ortho.astype(jnp.bfloat16)
     ortho_rows = lax.all_gather(ortho_half, "gene", axis=1, tiled=True)
     partial_value = loadings_of(ortho_rows)
-    next_basis = lax.psum(partial_value, "cell").astype(jnp.bfloat16)
+
+    def outputs_carry(original, axis_id="cell"):
+        return jnp.sum(lax.all_gather(original, axis_id), axis=0)
+
+    next_basis = outputs_carry(partial_value).astype(jnp.bfloat16)
     ortho_two = orthonormal(scores_of(next_basis), first_total)
     scale = jnp.sqrt(jnp.float32(lax.axis_size("cell") * cell_dev))
     ortho_two_half = ortho_two.astype(jnp.bfloat16)

time: 351 us -> 389 us (1.11)
  waiting for transfers between devices: 90.3 us -> 204 us
  blocking collectives: 169 us -> 87 us
  other arithmetic: 53.9 us -> 57.8 us
    all_gather x0 -> x1, waiting for transfers between devices: none -> 112 us  [outputs_carry(): return jnp.sum(lax.all_gather(original, axis_id), axis=0)]
    psum x1 -> x0, blocking collectives: 81.7 us -> none  [local(): next_basis = lax.psum(partial_value, 'cell').astype(jnp.bfloat16)]
    reduce_sum x0 -> x1, other arithmetic: none -> 3.96 us  [outputs_carry(): return jnp.sum(lax.all_gather(original, axis_id), axis=0)]
  transfers between devices with their start and end apart: 3 -> 4, of which waited for: 3 -> 4; matrix products, arithmetic and copies ran while one was open for 0% -> 0% of each run, Pallas kernels for 0% -> 0%
where the time goes in v1:
time: 389 us; the launch traced here: 388 us
  waiting for transfers between devices  204 us (52%)
  blocking collectives  87 us (22%)
  other arithmetic  57.8 us (15%)
  matrix products  14.9 us (4%)
  between operations  14.7 us (4%)
  local copies, waits for them, and re-layouts  8.59 us (2%)
    all_gather x1, waiting for transfers between devices, outputs_carry(): return jnp.sum(lax.all_gather(original, axis_id), axis=0)  112 us
    psum x2, blocking collectives, first_total(): return lax.psum(gram, ('cell', 'gene'))  81.3 us
    reduce_scatter x1, waiting for transfers between devices, local(): lax.psum_scatter(loadings_of(final_rows), 'cell', scatter_dimension=1, ti...  75.5 us
    reduce_scatter x2, waiting for transfers between devices, merge_halves(): lax.psum_scatter(partial_scores, 'gene', scatter_dimension=1, tiled=True)  16.5 us
    scatter-add x2, other arithmetic, scores_of(): jax.ops.segment_sum(products, row_target, num_segments=row_blocks + 1)  14.1 us
    scatter-add x2, other arithmetic, loadings_of(): jax.ops.segment_sum(products, col_target, num_segments=gene_blocks + 1)  14.1 us
    another operation x6, other arithmetic, orthonormal(): lower_one = jnp.linalg.cholesky(first)  13 us
    another operation x4, other arithmetic, solve_lower(): return lax.linalg.triangular_solve(lower, right, left_side=True, lower=True)  11.1 us
  transfers between devices with their start and end apart: 4, of which 4 were waited for; matrix products, arithmetic and copies ran while one was open for 0% of the time, Pallas kernels for 0%

profile of v1, /device:TPU:0, one launch (start us, length us, event | category | flops | bytes accessed | tf_op | source)
XLA Modules:
  0.0 387.7 jit_solution(13416190212108797483)
XLA Ops:
  11.2 2.9 fusion.6
  14.1 7.1 %scatter_fusion = f32[9,64,128]{2,1,0:T(8,128)S(1)} fusion(f32[9,64,128]{2,1,0:T(8,128)S(1)} %broadcast.69.clone, s32[64]{0:T(128)S(1)} %get-tuple-element.8, f32[64,64,128]{2,1,0:T(8,128)} %fusion.6), kind=kCustom, calls=%fused_computation.4 | custom fusion | flops 524288 | bytes 6291712 | tf_op jit(solution)/shard_map/scatter-add | solution.py:51
  22.0 10.5 %reduce-scatter.4.cloned.1.call-done = f32[64,512]{1,0:T(8,128)} async-done(((f32[64,1024]{1,0:T(8,128)}), f32[64,512]{1,0:T(8,128)}) %reduce-scatter.4.cloned.1.call-update) | async-done | bytes 131088 | tf_op jit(solution)/shard_map/reduce_scatter | solution.py:44
  32.5 1.2 fusion.40
  33.8 40.5 %psum.14 = f32[64,64]{0,1:T(8,128)S(1)} all-reduce(f32[64,64]{0,1:T(8,128)S(1)} %fusion.40), channel_id=1, replica_groups=mesh['cell'=16,'gene'=2] {'cell','gene'}, use_global_device_ids=true, to_apply=%region_2.4 | all-reduce | flops 4096 | bytes 32768 | tf_op jit(solution)/shard_map/psum | solution.py:41
  74.4 5.8 %cholesky.44 = f32[64,64]{1,0:T(8,128)S(1)} custom-call(f32[64,64]{1,0:T(8,128)S(1)} %fusion.30), custom_call_target="Cholesky" | custom-call | tf_op jit(solution)/shard_map/jit(cholesky)/cholesky | solution.py:21
  81.6 4.9 %custom-call.6 = f32[1,64,64]{1,2,0:T(8,128)S(1)} custom-call(f32[1,64,64]{2,1,0:T(8,128)S(1)} %fusion.24), custom_call_target="InvertDiagBlocksLowerTriangular" | custom-call | tf_op jit(solution)/shard_map/triangular_solve/custom-call.0 | solution.py:10
  87.7 1.9 all_gather.12
  90.4 2.1 fusion.4
  92.6 7.1 %scatter_fusion.1 = f32[17,64,128]{2,1,0:T(8,128)S(1)} fusion(f32[17,64,128]{2,1,0:T(8,128)S(1)} %broadcast.70.clone, s32[64]{0:T(128)S(1)} %get-tuple-element.9, f32[64,64,128]{2,1,0:T(8,128)} %fusion.4), kind=kCustom, calls=%fused_computation.5 | custom fusion | flops 524288 | bytes 6291712 | tf_op jit(solution)/shard_map/scatter-add | solution.py:59
  101.0 112.3 %all-gather.2.cloned.1.call-done = f32[16,64,2048]{2,1,0:T(8,128)} async-done(((f32[1,64,2048]{2,1,0:T(8,128)}), f32[16,64,2048]{2,1,0:T(8,128)}) %all-gather.2.cloned.1.call-update) | async-done | bytes 8388624 | tf_op jit(solution)/shard_map/all_gather | solution.py:70
  213.3 4.0 %reduce_sum.9 = bf16[64,2048]{1,0:T(8,128)(2,1)S(1)} reduce(f32[16,64,2048]{2,1,0:T(8,128)} %all-gather.2.cloned.1.call-done, f32[]{:T(128)} %constant.55.clone.1), dimensions={0}, to_apply=%region_6.11 | reduce | flops 1966080 | bytes 8650756 | tf_op jit(solution)/shard_map/reduce_sum | solution.py:70
  218.1 2.9 fusion.2
  221.0 7.1 %scatter_fusion.2 = f32[9,64,128]{2,1,0:T(8,128)S(1)} fusion(f32[9,64,128]{2,1,0:T(8,128)S(1)} %broadcast.69, s32[64]{0:T(128)S(1)} %get-tuple-element.8, f32[64,64,128]{2,1,0:T(8,128)} %fusion.2), kind=kCustom, calls=%fused_computation.6 | custom fusion | flops 524288 | bytes 6291712 | tf_op jit(solution)/shard_map/scatter-add | solution.py:51
  228.9 6.0 %reduce-scatter.6.cloned.1.call-done = f32[64,512]{1,0:T(8,128)} async-done(((f32[64,1024]{1,0:T(8,128)}), f32[64,512]{1,0:T(8,128)}) %reduce-scatter.6.cloned.1.call-update) | async-done | bytes 131088 | tf_op jit(solution)/shard_map/reduce_scatter | solution.py:44
  236.1 40.8 %psum.15 = f32[64,64]{0,1:T(8,128)S(1)} all-reduce(f32[64,64]{0,1:T(8,128)S(1)} %fusion.41), channel_id=1, replica_groups=mesh['cell'=16,'gene'=2] {'cell','gene'}, use_global_device_ids=true, to_apply=%region_9.14 | all-reduce | flops 4096 | bytes 32768 | tf_op jit(solution)/shard_map/psum | solution.py:41
  277.0 5.8 %cholesky.55 = f32[64,64]{1,0:T(8,128)S(1)} custom-call(f32[64,64]{1,0:T(8,128)S(1)} %fusion.28), custom_call_target="Cholesky" | custom-call | tf_op jit(solution)/shard_map/jit(cholesky)/cholesky | solution.py:21
  284.2 4.9 %custom-call.7 = f32[1,64,64]{1,2,0:T(8,128)S(1)} custom-call(f32[1,64,64]{2,1,0:T(8,128)S(1)} %fusion.25), custom_call_target="InvertDiagBlocksLowerTriangular" | custom-call | tf_op jit(solution)/shard_map/triangular_solve/custom-call.0 | solution.py:10
  289.1 1.2 fusion.39
  290.3 1.9 all_gather.15
  293.0 2.1 fusion
  295.1 7.1 %scatter_fusion.3 = f32[17,64,128]{2,1,0:T(8,128)S(1)} fusion(f32[17,64,128]{2,1,0:T(8,128)S(1)} %broadcast.70, s32[64]{0:T(128)S(1)} %get-tuple-element.9, f32[64,64,128]{2,1,0:T(8,128)} %fusion), kind=kCustom, calls=%fused_computation.7 | custom fusion | flops 524288 | bytes 6291712 | tf_op jit(solution)/shard_map/scatter-add | solution.py:59
  303.1 1.9 all_gather.14
  305.0 75.5 %reduce-scatter.8.cloned.1.call-done = f32[64,128]{1,0:T(8,128)} async-done(((f32[64,2048]{1,0:T(8,128)}), f32[64,128]{1,0:T(8,128)}) %reduce-scatter.8.cloned.1.call-update) | async-done | bytes 32784 | tf_op jit(solution)/shard_map/reduce_scatter | solution.py:81
  (52 shorter events, 15.5 us)
Async XLA Ops:
  7.2 4.0 %copy-start = (bf16[1,64,128,128]{3,2,1,0:T(8,128)(2,1)S(1)}, bf16[1,64,128,128]{3,2,1,0:T(8,128)(2,1)}, u32[]{:S(2)}) copy-start(bf16[1,64,128,128]{3,2,1,0:T(8,128)(2,1)} %param.12) | copy-start | bytes 6291460
  7.2 4.0 %copy-start.1 = (s32[1,64]{1,0:T(1,128)S(1)}, s32[1,64]{1,0:T(1,128)}, u32[]{:S(2)}) copy-start(s32[1,64]{1,0:T(1,128)} %param.14) | copy-start | bytes 772
  7.2 4.0 %copy-start.2 = (s32[1,64]{1,0:T(1,128)S(1)}, s32[1,64]{1,0:T(1,128)}, u32[]{:S(2)}) copy-start(s32[1,64]{1,0:T(1,128)} %param.13) | copy-start | bytes 772
  7.2 25.3 %reduce-scatter.4.cloned.1.call-start = ((), (), s32[]{:S(2)}) async-start(), calls=%async_computation.3 | async-start | bytes 393216 | tf_op jit(solution)/shard_map/reduce_scatter | solution.py:44
  21.9 191.4 %all-gather.2.cloned.1.call-start = ((), (), s32[]{:S(2)}) async-start(), calls=%async_computation.4 | async-start | bytes 8912896 | tf_op jit(solution)/shard_map/all_gather | solution.py:70
  100.9 133.9 %reduce-scatter.6.cloned.1.call-start = ((), (), s32[]{:S(2)}) async-start(), calls=%async_computation.5 | async-start | bytes 393216 | tf_op jit(solution)/shard_map/reduce_scatter | solution.py:44
  228.8 151.7 %reduce-scatter.8.cloned.1.call-start = ((), (), s32[]{:S(2)}) async-start(), calls=%async_computation.6 | async-start | bytes 557056 | tf_op jit(solution)/shard_map/reduce_scatter | solution.py:81
Sparse Core Ops, SparseCore 0:
  22.0 10.4 reduce-scatter.3
  101.1 112.1 all-gather.1
  228.9 5.9 reduce-scatter.5
  303.2 77.2 reduce-scatter.7
